TPU v7x, 128 devices: a whole 4x4x4 slice. The times are simulated.
128 devices in a mesh: cp: 64 (over x, z, y), hd: 2 (over core).
Axes of the slice: x: 4, y: 4, z: 4, core: 2. Of those that a mesh axis runs over, the one named last changes fastest.
Arguments:
- queries: bfloat16 [12288, 4096], P('cp', 'hd'), may hold values from -48 to 48
- keys: bfloat16 [12288, 1024], P('cp', 'hd'), may hold values from -48 to 48
- values: bfloat16 [12288, 1024], P('cp', 'hd'), may hold values from -6 to 6
- span_table: int32 [128], replicated, may hold values from 0 to 127, as said below
- doc_ids: int32 [12288], replicated, may hold values from 0 to 7, never falling along the last dimension, each value on 1 to 3072 neighbouring positions
- out_weight: bfloat16 [4096, 4096], P('hd'), may hold values from -0.09375 to 0.09375
Outputs:
- mixed: bfloat16 [12288, 4096], P(('cp', 'hd'))
Inputs may be any that keep to these rules, and one draw needn't show every extreme that they name: `span_table`: slots 2 j and 2 j + 1 hold two spans c and 127 - c, and every span is held once.
All inputs are finite; a program needn't handle non-finite values.
Results may differ from a plain program's by a relative error of at most 0.0095.
Values may be sent and summed in bfloat16 or wider, within the bound.
A program may use at most 128 MiB of HBM per device.

v0:
```python
import jax
import jax.numpy as jnp
from jax import lax
from jax.experimental import pallas as pl
from jax.experimental.pallas import tpu as pltpu
from jax.sharding import PartitionSpec as P

HEAD = 128
SPAN = 96
ROWS = 192
GROUP = 512
SLOTS = 64
KEYS = 12288
BLOCK = 384
MESH = pl.DeviceIdType.MESH
NEG = -1e30


def place():
    cp = lax.axis_index("cp")
    core = lax.axis_index("hd")
    x = cp // 16
    z = (cp // 4) % 4
    y = cp % 4
    band = z // 2
    cross = (band - core) * (band - core)
    return cp, core, x, z, y, band, cross


def chip(x, z, y):
    return x * 16 + z * 4 + y


def enter_group(x, z, y, core, others):
    barrier = pltpu.get_barrier_semaphore()
    count = 0
    for dz in range(2):
        zz = z if dz == 0 else 3 - z
        for dy in range(4):
            for dc in range(2):
                if dz + dy + dc == 0:
                    continue
                target = (chip(x, zz, (y + dy) % 4), (core + dc) % 2)
                pl.semaphore_signal(barrier, inc=1, device_id=target, device_id_type=MESH)
                count += 1
    for target in others:
        pl.semaphore_signal(barrier, inc=1, device_id=target, device_id_type=MESH)
        count += 1
    pl.semaphore_wait(barrier, count)


def spread_kernel(
    q_ref, k_ref, v_ref, qr_ref, kv_ref, ex_send, ex_recv, q_send, q_recv, ag_send, ag_recv, dd_send, dd_recv
):
    cp, core, x, z, y, band, cross = place()
    zo = 3 - z
    za = z + 1 - 2 * (z % 2)
    zao = 3 - za
    xr, xl, xo = (x + 1) % 4, (x + 3) % 4, (x + 2) % 4
    right = (chip(xr, z, y), core)
    left = (chip(xl, z, y), core)
    across = (chip(x, za, y), core)
    twin = (cp, 1 - core)
    enter_group(x, z, y, core, (right, left, across))

    zt = z + cross * (3 - 2 * z)
    finish = []

    def push(src, dst, device, send_sem, recv_sem, own):
        copy = pltpu.make_async_remote_copy(
            src_ref=src, dst_ref=dst, send_sem=send_sem, recv_sem=recv_sem, device_id=device, device_id_type=MESH
        )
        if own is None:
            copy.start()
            finish.append((None, copy))
            return

        @pl.when(own)
        def _():
            pltpu.make_async_copy(src, dst, recv_sem).start()

        @pl.when(jnp.logical_not(own))
        def _():
            copy.start()

        finish.append((own, copy))

    for dy in range(4):
        yy = (y + dy) % 4
        home = chip(x, zt, yy)
        cols = pl.ds(pl.multiple_of(yy * HEAD, HEAD), HEAD)
        for t, ref in enumerate((k_ref, v_ref)):
            own = (cross + jnp.abs(core - t) == 0) if dy == 0 else None
            push(
                ref.at[:, cols],
                kv_ref.at[t, cp],
                (home, t),
                ex_send.at[dy * 2 + t],
                ex_recv.at[cross],
                own,
            )
    keeper = core + cross * (1 - 2 * core)

    def query_copy(dy):
        yy = (y + dy) % 4
        cols = pl.ds(pl.multiple_of(yy * GROUP, GROUP), GROUP)
        return pltpu.make_async_remote_copy(
            src_ref=q_ref.at[:, cols],
            dst_ref=qr_ref.at[y],
            send_sem=q_send.at[dy],
            recv_sem=q_recv,
            device_id=(chip(x, zt, yy), keeper),
            device_id_type=MESH,
        )

    def send_queries():
        @pl.when(cross == 0)
        def _():
            cols = pl.ds(pl.multiple_of(y * GROUP, GROUP), GROUP)
            pltpu.make_async_copy(q_ref.at[:, cols], qr_ref.at[y], q_recv).start()

        @pl.when(cross != 0)
        def _():
            query_copy(0).start()

        for dy in range(1, 4):
            query_copy(dy).start()

    def part(t, xs, zs):
        return kv_ref.at[t, pl.ds(xs * 16 + zs * 4, 4)]

    def arrive(t, xs, zs, sem):
        ref = part(t, xs, zs)
        pltpu.make_async_copy(ref, ref, sem).wait()

    def run(t, steps):
        sends = []
        for turn, (kind, xs, zs, targets) in enumerate(steps):
            if turn == 2:
                send_queries()
            if kind == "own":
                arrive(t, xs, zs, ex_recv.at[0])
            elif kind == "pair":
                arrive(t, xs, zs, ex_recv.at[1])
            else:
                arrive(t, xs, zs, ag_recv.at[xs * 4 + zs])
            for device in targets:
                copy = pltpu.make_async_remote_copy(
                    src_ref=part(t, xs, zs),
                    dst_ref=part(t, xs, zs),
                    send_sem=ag_send.at[len(sends)],
                    recv_sem=ag_recv.at[xs * 4 + zs],
                    device_id=device,
                    device_id_type=MESH,
                )
                copy.start()
                sends.append(copy)
            copy = pltpu.make_async_remote_copy(
                src_ref=part(t, xs, zs),
                dst_ref=part(t, xs, zs),
                send_sem=dd_send.at[xs * 4 + zs],
                recv_sem=dd_recv.at[xs * 4 + zs],
                device_id=twin,
                device_id_type=MESH,
            )
            copy.start()
        for copy in sends:
            copy.wait_send()

    @pl.when(core == 0)
    def _():
        run(
            0,
            (
                ("own", x, z, (across, right, left)),
                ("pair", x, zo, (across, left, right)),
                ("got", x, za, (right, left)),
                ("got", x, zao, (left, right)),
                ("got", xl, z, (right,)),
                ("got", xr, z, ()),
                ("got", xr, zo, (left,)),
                ("got", xl, zo, ()),
                ("got", xl, za, (right,)),
                ("got", xr, za, ()),
                ("got", xr, zao, (left,)),
                ("got", xl, zao, ()),
                ("got", xo, z, ()),
                ("got", xo, zo, ()),
                ("got", xo, za, ()),
                ("got", xo, zao, ()),
            ),
        )

    @pl.when(core == 1)
    def _():
        run(
            1,
            (
                ("own", x, z, (right, left, across)),
                ("pair", x, zo, (left, right, across)),
                ("got", xl, z, (right, across)),
                ("got", xr, z, (across,)),
                ("got", xr, zo, (left, across)),
                ("got", xl, zo, (across,)),
                ("got", x, za, ()),
                ("got", x, zao, ()),
                ("got", xo, z, (across,)),
                ("got", xo, zo, (across,)),
                ("got", xl, za, ()),
                ("got", xr, za, ()),
                ("got", xr, zao, ()),
                ("got", xl, zao, ()),
                ("got", xo, za, ()),
                ("got", xo, zao, ()),
            ),
        )

    for piece in range(16):
        ref = kv_ref.at[1 - core, pl.ds(piece * 4, 4)]
        pltpu.make_async_copy(ref, ref, dd_recv.at[piece]).wait()
        ref = kv_ref.at[core, pl.ds(piece * 4, 4)]
        pltpu.make_async_copy(ref, ref, dd_send.at[piece]).wait()
    pltpu.make_async_copy(qr_ref, qr_ref, q_recv).wait()

    @pl.when(cross != 0)
    def _():
        query_copy(0).wait_send()

    for dy in range(1, 4):
        query_copy(dy).wait_send()

    for own, copy in finish:
        if own is None:
            copy.wait_send()
        else:

            @pl.when(jnp.logical_not(own))
            def _():
                copy.wait_send()


def spread(queries, keys, values):
    return pl.pallas_call(
        spread_kernel,
        out_shape=(
            jax.ShapeDtypeStruct((4, ROWS, GROUP), jnp.bfloat16),
            jax.ShapeDtypeStruct((2, SLOTS, ROWS, HEAD), jnp.bfloat16),
        ),
        in_specs=[pl.BlockSpec(memory_space=pltpu.HBM)] * 3,
        out_specs=[pl.BlockSpec(memory_space=pltpu.VMEM)] * 2,
        scratch_shapes=[
            pltpu.SemaphoreType.DMA((8,)),
            pltpu.SemaphoreType.DMA((2,)),
            pltpu.SemaphoreType.DMA((4,)),
            pltpu.SemaphoreType.DMA,
            pltpu.SemaphoreType.DMA((14,)),
            pltpu.SemaphoreType.DMA((16,)),
            pltpu.SemaphoreType.DMA((16,)),
            pltpu.SemaphoreType.DMA((16,)),
        ],
        compiler_params=pltpu.CompilerParams(
            collective_id=0, has_side_effects=True, vmem_limit_bytes=8 * 1024 * 1024
        ),
        cost_estimate=pl.CostEstimate(flops=20_000_000_000, bytes_accessed=40_000_000, transcendentals=0),
        name="spread",
    )(queries, keys, values)


WIDTH = 4 * SPAN
ITEMS = 96
UNROLL = 8
HUGE = 2.0**100
FACTOR = HEAD ** (-0.5) * 1.4426950408889634


def attend_kernel(
    span_ref, doc_ref, q_ref, kv_ref, o_ref, slot_ref, item_q, item_low, item_first, qa_ref, s_ref, p_ref, acc_ref
):
    cp, core, x, z, y, band, cross = place()
    zs = z + cross * (3 - 2 * z)

    def invert(slot, carry):
        slot_ref[span_ref[slot]] = slot
        return carry

    lax.fori_loop(0, 2 * SLOTS, invert, 0, unroll=8)
    docs = doc_ref[...]
    starts = [jnp.int32(0)]
    starts += [jnp.sum((docs < d).astype(jnp.float32)).astype(jnp.int32) for d in range(1, 8)]
    ends = starts[1:] + [jnp.int32(KEYS)]
    lane = lax.broadcasted_iota(jnp.int32, (1, HEAD), 1)
    start = jnp.where(lane == 104, -KEYS, KEYS)
    end = jnp.zeros((1, HEAD), jnp.int32)
    for d in range(8):
        start = jnp.where(lane == d, starts[d], start)
        end = jnp.where(lane == d, ends[d], end)

    def record(at, index, low, first):
        item_q[at] = index
        item_low[at] = low
        item_first[at] = first

    row = lax.broadcasted_iota(jnp.int32, (SPAN, HEAD), 0)
    col = lax.broadcasted_iota(jnp.int32, (SPAN, HEAD), 1)
    later = ((col >= 8) & (col < 104) & (col - 8 > row)) | (col == 104)
    later = jnp.where(later, -HUGE, 0.0)
    reach = jnp.where(lane < 8, start, -KEYS)
    limit = jnp.where(lane < 8, end, 2 * KEYS)
    heads = [(begin, begin // SPAN) for begin in starts]

    def plan(index, at):
        span = span_ref[2 * chip(x, zs, index // 2) + index % 2]
        first = span * SPAN
        same = (row >= reach - first) & (row < limit - first)
        qa_ref[index] = jnp.where(same, later, -HUGE).astype(jnp.bfloat16)
        acc_ref[index] = jnp.zeros((HEAD + 16, WIDTH), jnp.float32)
        lowest = jnp.int32(0)
        for begin, head in heads[1:]:
            lowest = jnp.where(first >= begin, head, lowest)
        for turn in range(9):
            record(at + turn, index, span - 3 - 4 * turn, 1 if turn == 0 else 0)
        return at + ((span - lowest + 4) >> 2)

    for at in range(2):
        record(at, 8, 0, 0)
    total = lax.fori_loop(0, 8, plan, jnp.int32(2))
    for at in range(UNROLL + 2):
        record(total + at, 8, 0, 0)
    s_ref[1] = jnp.zeros((BLOCK, WIDTH), jnp.float32)
    p_ref[0] = jnp.zeros((BLOCK, WIDTH), jnp.bfloat16)
    acc_ref[8] = jnp.zeros((HEAD + 16, WIDTH), jnp.float32)
    qa_ref[8] = jnp.zeros((SPAN, HEAD), jnp.bfloat16)
    row = lax.broadcasted_iota(jnp.int32, (BLOCK, HEAD), 0)
    col = lax.broadcasted_iota(jnp.int32, (BLOCK, HEAD), 1)
    corner = jnp.where(row >= BLOCK - SPAN, row - (BLOCK - SPAN) + 8, -1)

    def fetch(which, low):
        slots = [slot_ref[jnp.maximum(low + j, 0)] for j in range(4)]
        return jnp.concatenate([kv_ref[which, slot] for slot in slots], axis=0)

    def step(at, parity, state):
        best, fade = state
        low = item_low[at + 2]
        base = low * SPAN
        seen = (row >= start - base) & (row < end - base)
        seen = seen | (corner + (1 - item_first[at + 2]) * 4096 == col)
        extra = jnp.where(seen, 1.0, 0.0).astype(jnp.bfloat16)
        keys = jnp.concatenate([fetch(0, low), extra], axis=1)
        index = item_q[at + 2]
        source = jnp.minimum(index, 7)
        rows = pl.ds(pl.multiple_of((source % 2) * SPAN, SPAN), SPAN)
        q = q_ref[source // 2, rows, :]
        q = jnp.concatenate([q[:, h * HEAD : (h + 1) * HEAD] for h in range(4)], axis=0)
        q = jnp.concatenate([q, jnp.concatenate([qa_ref[index]] * 4, axis=0)], axis=1)
        s_ref[parity] = lax.dot_general(keys, q, (((1,), (1,)), ((), ())), preferred_element_type=jnp.float32)

        s = s_ref[1 - parity]
        best = jnp.where(item_first[at + 1] == 1, NEG, best)
        new = jnp.maximum(best, jnp.max(s, axis=0, keepdims=True))
        p_ref[1 - parity] = jnp.exp2(s * FACTOR - new * FACTOR).astype(jnp.bfloat16)

        v = fetch(1, item_low[at])
        v = jnp.concatenate([v.T, jnp.ones((16, BLOCK), jnp.bfloat16)], axis=0)
        index = item_q[at]
        acc_ref[index] = acc_ref[index] * fade + jnp.dot(v, p_ref[parity], preferred_element_type=jnp.float32)
        return new, jnp.exp2((best - new) * FACTOR)

    def several(turn, state):
        for k in range(UNROLL):
            state = step(UNROLL * turn + k, k % 2, state)
        return state

    turns = total // UNROLL
    state = (jnp.full((1, WIDTH), NEG, jnp.float32), jnp.zeros((1, WIDTH), jnp.float32))
    state = lax.fori_loop(0, turns, several, state)

    def couple(turn, state):
        for k in range(2):
            state = step(UNROLL * turns + 2 * turn + k, k, state)
        return state

    lax.fori_loop(0, (total - UNROLL * turns + 1) >> 1, couple, state)

    def finish(index, carry):
        rows = pl.ds(pl.multiple_of((index % 2) * SPAN, SPAN), SPAN)
        out = (acc_ref[index, 0:HEAD] * (1.0 / acc_ref[index, HEAD : HEAD + 1])).T.astype(jnp.bfloat16)
        for h in range(4):
            o_ref[index // 2, rows, h * HEAD : (h + 1) * HEAD] = out[h * SPAN : (h + 1) * SPAN]
        return carry

    lax.fori_loop(0, 8, finish, 0)


def attend(span_table, doc_ids, q, kv):
    return pl.pallas_call(
        attend_kernel,
        out_shape=jax.ShapeDtypeStruct((4, ROWS, GROUP), jnp.bfloat16),
        in_specs=[
            pl.BlockSpec(memory_space=pltpu.SMEM),
            pl.BlockSpec(memory_space=pltpu.VMEM),
            pl.BlockSpec(memory_space=pltpu.VMEM),
            pl.BlockSpec(memory_space=pltpu.VMEM),
        ],
        out_specs=pl.BlockSpec(memory_space=pltpu.VMEM),
        scratch_shapes=[
            pltpu.SMEM((2 * SLOTS,), jnp.int32),
            pltpu.SMEM((ITEMS,), jnp.int32),
            pltpu.SMEM((ITEMS,), jnp.int32),
            pltpu.SMEM((ITEMS,), jnp.int32),
            pltpu.VMEM((9, SPAN, HEAD), jnp.bfloat16),
            pltpu.VMEM((2, BLOCK, WIDTH), jnp.float32),
            pltpu.VMEM((2, BLOCK, WIDTH), jnp.bfloat16),
            pltpu.VMEM((9, HEAD + 16, WIDTH), jnp.float32),
        ],
        compiler_params=pltpu.CompilerParams(vmem_limit_bytes=24 * 1024 * 1024),
        name="attend",
    )(span_table, doc_ids.reshape(KEYS // 128, 128), q, kv.reshape(2, 2 * SLOTS, SPAN, HEAD))


CHUNK = 512
CHUNKS = 8


def project_kernel(
    o_ref, w_ref, out_ref, attn, weight, partial, share, theirs, w_sem, b_send, b_recv, s_send, s_recv
):
    cp, core, x, z, y, band, cross = place()
    for n in range(CHUNKS):
        pltpu.make_async_copy(w_ref.at[:, pl.ds(n * CHUNK, CHUNK)], weight.at[n], w_sem.at[n]).start()
    zs = z + cross * (3 - 2 * z)
    barrier = pltpu.get_barrier_semaphore()
    pl.semaphore_signal(barrier, inc=1, device_id=(cp, 1 - core), device_id_type=MESH)
    for dy in range(1, 4):
        pl.semaphore_signal(barrier, inc=1, device_id=(chip(x, zs, (y + dy) % 4), band), device_id_type=MESH)

    @pl.when(cross != 0)
    def _():
        pl.semaphore_signal(barrier, inc=1, device_id=(chip(x, zs, y), band), device_id_type=MESH)

    pl.semaphore_wait(barrier, 4 + cross)
    copies = []
    for dy in (0, 1, 3, 2):
        yy = (y + dy) % 4
        src, dst = o_ref.at[yy], attn.at[y]
        copy = pltpu.make_async_remote_copy(
            src_ref=src,
            dst_ref=dst,
            send_sem=b_send.at[dy],
            recv_sem=b_recv.at[y],
            device_id=(chip(x, zs, yy), band),
            device_id_type=MESH,
        )
        copies.append(copy)
        if dy == 0:

            @pl.when(cross == 0)
            def _():
                pltpu.make_async_copy(src, dst, b_recv.at[y]).start()

            @pl.when(cross != 0)
            def _():
                copy.start()
        else:
            copy.start()
    mine = pl.ds(pl.multiple_of(core * SPAN, SPAN), SPAN)
    yours = pl.ds(pl.multiple_of((1 - core) * SPAN, SPAN), SPAN)

    def give(n):
        return pltpu.make_async_remote_copy(
            src_ref=share.at[n, yours],
            dst_ref=theirs.at[n],
            send_sem=s_send.at[n],
            recv_sem=s_recv.at[n],
            device_id=(cp, 1 - core),
            device_id_type=MESH,
        )

    def gain(k, n):
        rows = pl.ds(pl.multiple_of(k * GROUP, GROUP), GROUP)
        return jnp.dot(attn[k], weight[n, rows, :], preferred_element_type=jnp.float32)

    for n in range(CHUNKS):
        pltpu.make_async_copy(weight.at[n], weight.at[n], w_sem.at[n]).wait()
    def block(dy):
        return (y + dy) % 4

    def await_block(dy):
        pltpu.make_async_copy(attn.at[block(dy)], attn.at[block(dy)], b_recv.at[block(dy)]).wait()

    for dy in (0, 3, 1):
        await_block(dy)
    for n in range(CHUNKS):
        partial[n] = gain(block(0), n) + gain(block(3), n) + gain(block(1), n)
    await_block(2)
    for n in range(CHUNKS):
        share[n] = (partial[n] + gain(block(2), n)).astype(jnp.bfloat16)
        give(n).start()

    def add(n, carry):
        give(n).wait()
        cols = pl.ds(pl.multiple_of(n * CHUNK, CHUNK), CHUNK)
        total = share[n, mine, :].astype(jnp.float32) + theirs[n].astype(jnp.float32)
        out_ref[:, cols] = total.astype(jnp.bfloat16)
        return carry

    lax.fori_loop(0, CHUNKS, add, 0)
    for turn, copy in enumerate(copies):
        if turn == 0:

            @pl.when(cross != 0)
            def _():
                copy.wait_send()
        else:
            copy.wait_send()


def project(o, weight):
    return pl.pallas_call(
        project_kernel,
        out_shape=jax.ShapeDtypeStruct((SPAN, 4096), jnp.bfloat16),
        in_specs=[pl.BlockSpec(memory_space=pl.ANY), pl.BlockSpec(memory_space=pltpu.HBM)],
        out_specs=pl.BlockSpec(memory_space=pltpu.VMEM),
        scratch_shapes=[
            pltpu.VMEM((4, ROWS, GROUP), jnp.bfloat16),
            pltpu.VMEM((CHUNKS, 2048, CHUNK), jnp.bfloat16),
            pltpu.VMEM((CHUNKS, ROWS, CHUNK), jnp.float32),
            pltpu.VMEM((CHUNKS, ROWS, CHUNK), jnp.bfloat16),
            pltpu.VMEM((CHUNKS, SPAN, CHUNK), jnp.bfloat16),
            pltpu.SemaphoreType.DMA((CHUNKS,)),
            pltpu.SemaphoreType.DMA((4,)),
            pltpu.SemaphoreType.DMA((4,)),
            pltpu.SemaphoreType.DMA((CHUNKS,)),
            pltpu.SemaphoreType.DMA((CHUNKS,)),
        ],
        compiler_params=pltpu.CompilerParams(
            collective_id=1, has_side_effects=True, vmem_limit_bytes=32 * 1024 * 1024
        ),
        name="project",
    )(o, weight)


def local(queries, keys, values, span_table, doc_ids, out_weight):
    far = lambda value: pltpu.with_memory_space_constraint(value, pltpu.HBM)
    q, kv = spread(far(queries), far(keys), far(values))
    o = attend(span_table, doc_ids, q, kv)
    return project(o, far(out_weight))


def solution(mesh):
    return jax.shard_map(
        local,
        mesh=mesh,
        in_specs=(P("cp", "hd"), P("cp", "hd"), P("cp", "hd"), P(), P(), P("hd", None)),
        out_specs=P(("cp", "hd"), None),
        check_vma=False,
    )
```

profile of v0, /device:TPU:1, one launch (start us, length us, event | category | flops | bytes accessed | tf_op | source)
XLA Modules:
  0.0 73.2 jit_solution(5939381413631322657)
XLA Ops:
  0.0 0.0 copy-start
  0.0 0.0 copy-start.1
  0.0 39.3 %spread.1 = (bf16[4,192,512]{2,1,0:T(8,128)(2,1)S(1)}, bf16[2,64,192,128]{3,2,1,0:T(8,128)(2,1)S(1)}) custom-call(bf16[192,2048]{1,0:T(8,128)(2,1)} %q_ref.1, bf16[192,512]{1,0:T(8,128)(2,1)} %k_ref.1, bf16[192,512]{1,0:T(8,128)(2,1)} %v_ref.1), custom_call_target="tpu_custom_call" | custom-call | flops 20000000000 | bytes 40000000 | tf_op jit(solution)/shard_map/spread/pallas_call | solution.py:243
  39.3 0.0 copy-done
  39.3 0.0 copy-done.1
  39.3 12.4 %attend.1.o_ref = bf16[4,192,512]{2,1,0:T(8,128)(2,1)S(1)} custom-call(s32[128]{0:T(128)S(1)} %copy-done.1, s32[96,128]{1,0:T(8,128)S(1)} %bitcast.3, bf16[4,192,512]{2,1,0:T(8,128)(2,1)S(1)} %get-tuple-element.7.q_ref, bf16[2,128,96,128]{3,2,1,0:T(8,128)(2,1)S(1)} %bitcast.2), custom_call_target="tpu_custom_call" | custom-call | tf_op jit(solution)/shard_map/attend/pallas_call | solution.py:395
  51.7 20.6 %project.1 = bf16[96,4096]{1,0:T(8,128)(2,1)S(1)} custom-call(bf16[4,192,512]{2,1,0:T(8,128)(2,1)S(1)} %attend.1.o_ref, bf16[2048,4096]{1,0:T(8,128)(2,1)} %w_ref.1), custom_call_target="tpu_custom_call" | custom-call | tf_op jit(solution)/shard_map/project/pallas_call | solution.py:518
  72.3 0.9 %copy.8 = bf16[96,4096]{1,0:T(8,128)(2,1)} copy(bf16[96,4096]{1,0:T(8,128)(2,1)S(1)} %project.1) | data formatting | bytes 1572864
Async XLA Ops:
  0.0 39.3 %copy-start = (s32[12288]{0:T(1024)S(1)}, s32[12288]{0:T(1024)}, u32[]{:S(2)}) copy-start(s32[12288]{0:T(1024)} %param.10) | copy-start | bytes 147460
  0.0 39.3 %copy-start.1 = (s32[128]{0:T(128)S(1)}, s32[128]{0:T(128)}, u32[]{:S(2)}) copy-start(s32[128]{0:T(128)} %span_ref.1) | copy-start | bytes 1540
where the time goes:
time: 73.7 us; the launch traced here: 73.2 us
  Pallas kernels  72.3 us (98%)
  local copies, waits for them, and re-layouts  0.89 us (1%)
    pallas_call x1, Pallas kernels, spread(): pl.pallas_call(spread_kernel, out_shape=(jax.ShapeDtypeStruct((4, ROWS, G...  39.3 us
    pallas_call x1, Pallas kernels, project(): pl.pallas_call(project_kernel, out_shape=jax.ShapeDtypeStruct((SPAN, 4096...  20.6 us
    pallas_call x1, Pallas kernels, attend(): pl.pallas_call(attend_kernel, out_shape=jax.ShapeDtypeStruct((4, ROWS, GR...  12.4 us

commit v1 on v0

--- a/solution.py
+++ b/solution.py
@@ -283,10 +283,12 @@
         slot_ref[span_ref[slot]] = slot
         return carry
 
-    lax.fori_loop(0, 2 * SLOTS, invert, 0, unroll=8)
+    lax.fori_loop(0, 2 * SLOTS, invert, 0, unroll=True)
     docs = doc_ref[...]
     starts = [jnp.int32(0)]
-    starts += [jnp.sum((docs < d).astype(jnp.float32)).astype(jnp.int32) for d in range(1, 8)]
+    counts = [jnp.sum((docs < d).astype(jnp.float32), axis=0, keepdims=True) for d in range(1, 8)]
+    counts = jnp.sum(jnp.concatenate(counts + [counts[0]], axis=0), axis=1, keepdims=True).astype(jnp.int32)
+    starts += [counts[d, 0] for d in range(7)]
     ends = starts[1:] + [jnp.int32(KEYS)]
     lane = lax.broadcasted_iota(jnp.int32, (1, HEAD), 1)
     start = jnp.where(lane == 104, -KEYS, KEYS)
@@ -323,7 +325,7 @@
 
     for at in range(2):
         record(at, 8, 0, 0)
-    total = lax.fori_loop(0, 8, plan, jnp.int32(2))
+    total = lax.fori_loop(0, 8, plan, jnp.int32(2), unroll=2)
     for at in range(UNROLL + 2):
         record(total + at, 8, 0, 0)
     s_ref[1] = jnp.zeros((BLOCK, WIDTH), jnp.float32)
@@ -388,7 +390,7 @@
             o_ref[index // 2, rows, h * HEAD : (h + 1) * HEAD] = out[h * SPAN : (h + 1) * SPAN]
         return carry
 
-    lax.fori_loop(0, 8, finish, 0)
+    lax.fori_loop(0, 8, finish, 0, unroll=4)
 
 
 def attend(span_table, doc_ids, q, kv):

time: 73.7 us -> 71.8 us (0.974)
  Pallas kernels: 72.3 us -> 70.3 us
    pallas_call x1, Pallas kernels: 12.4 us -> 10.7 us  [attend(): pl.pallas_call(attend_kernel, out_shape=jax.ShapeDtypeStruct((4, ROWS, GR...]
where the time goes in v1:
time: 71.8 us; the launch traced here: 71.2 us
  Pallas kernels  70.3 us (98%)
  local copies, waits for them, and re-layouts  0.89 us (1%)
    pallas_call x1, Pallas kernels, spread(): pl.pallas_call(spread_kernel, out_shape=(jax.ShapeDtypeStruct((4, ROWS, G...  39.3 us
    pallas_call x1, Pallas kernels, project(): pl.pallas_call(project_kernel, out_shape=jax.ShapeDtypeStruct((SPAN, 4096...  20.3 us
    pallas_call x1, Pallas kernels, attend(): pl.pallas_call(attend_kernel, out_shape=jax.ShapeDtypeStruct((4, ROWS, GR...  10.7 us

profile of v1, /device:TPU:1, one launch (start us, length us, event | category | flops | bytes accessed | tf_op | source)
XLA Modules:
  0.0 71.2 jit_solution(798412207920967285)
XLA Ops:
  0.0 0.0 copy-start
  0.0 0.0 copy-start.1
  0.0 39.3 %spread.1 = (bf16[4,192,512]{2,1,0:T(8,128)(2,1)S(1)}, bf16[2,64,192,128]{3,2,1,0:T(8,128)(2,1)S(1)}) custom-call(bf16[192,2048]{1,0:T(8,128)(2,1)} %q_ref.1, bf16[192,512]{1,0:T(8,128)(2,1)} %k_ref.1, bf16[192,512]{1,0:T(8,128)(2,1)} %v_ref.1), custom_call_target="tpu_custom_call" | custom-call | flops 20000000000 | bytes 40000000 | tf_op jit(solution)/shard_map/spread/pallas_call | solution.py:243
  39.3 0.0 copy-done
  39.3 0.0 copy-done.1
  39.3 10.7 %attend.1.o_ref = bf16[4,192,512]{2,1,0:T(8,128)(2,1)S(1)} custom-call(s32[128]{0:T(128)S(1)} %copy-done.1, s32[96,128]{1,0:T(8,128)S(1)} %bitcast.3, bf16[4,192,512]{2,1,0:T(8,128)(2,1)S(1)} %get-tuple-element.7.q_ref, bf16[2,128,96,128]{3,2,1,0:T(8,128)(2,1)S(1)} %bitcast.2), custom_call_target="tpu_custom_call" | custom-call | tf_op jit(solution)/shard_map/attend/pallas_call | solution.py:397
  50.0 20.3 %project.1 = bf16[96,4096]{1,0:T(8,128)(2,1)S(1)} custom-call(bf16[4,192,512]{2,1,0:T(8,128)(2,1)S(1)} %attend.1.o_ref, bf16[2048,4096]{1,0:T(8,128)(2,1)} %w_ref.1), custom_call_target="tpu_custom_call" | custom-call | tf_op jit(solution)/shard_map/project/pallas_call | solution.py:520
  70.3 0.9 %copy.8 = bf16[96,4096]{1,0:T(8,128)(2,1)} copy(bf16[96,4096]{1,0:T(8,128)(2,1)S(1)} %project.1) | data formatting | bytes 1572864
Async XLA Ops:
  0.0 39.3 %copy-start = (s32[12288]{0:T(1024)S(1)}, s32[12288]{0:T(1024)}, u32[]{:S(2)}) copy-start(s32[12288]{0:T(1024)} %param.10) | copy-start | bytes 147460
  0.0 39.3 %copy-start.1 = (s32[128]{0:T(128)S(1)}, s32[128]{0:T(128)}, u32[]{:S(2)}) copy-start(s32[128]{0:T(128)} %span_ref.1) | copy-start | bytes 1540
